TPU v7x, 32 devices: a whole 2x2x4 slice. The times are simulated.
32 devices in a mesh: dp: 4 (over y, x), expert: 8 (over z, core).
Axes of the slice: x: 2, y: 2, z: 4, core: 2. Of those that a mesh axis runs over, the one named last changes fastest.
Arguments:
- hidden: bfloat16 [49152, 1024], P(('dp', 'expert')), may hold values from -6 to 6
- dout: bfloat16 [49152, 7168], P(('dp', 'expert')), may hold values from -1536 to 1536
- counts: int32 [32, 256], P(('dp', 'expert')), may hold values from 1 to 1536, as said below
- bucket_expert: int32 [1], replicated, may hold values from 0 to 255
- param: float32 [1024, 7168], P(('dp', 'expert')), may hold values from -0.1875 to 0.1875
- momentum: float32 [1024, 7168], P(('dp', 'expert')), may hold values from -3 to 3
Outputs:
- new_param: float32 [1024, 7168], P(('dp', 'expert'))
- new_momentum: float32 [1024, 7168], P(('dp', 'expert'))
- direction: float32 [1024, 7168], P(('dp', 'expert'))
Inputs may be any that keep to these rules, and one draw needn't show every extreme that they name: `counts`: row k is device k's count; its rows k * 1536 + t with t below the count are live. For every expert some device has exactly 1536.
All inputs are finite; a program needn't handle non-finite values.
Results may differ from a plain program's by a relative error of at most 0.0003.
Values sent between devices are 32-bit elements; how exact they have to be, the bound alone decides.
A program may use at most 128 MiB of HBM per device.

v0:
```python
import jax
import jax.numpy as jnp
from jax import lax
from jax.sharding import PartitionSpec as P

first_beta = 0.9
second_beta = 0.99
decay_rate = 0.1
learn_rate = 0.001
soft_width = 0.05


def block_product(columns, dout):
    dims = (((0,), (0,)), ((), ()))
    return lax.dot_general(columns, dout, dims, preferred_element_type=jnp.float32)


def body(hidden, dout, counts, bucket_expert, param, momentum):
    rows_local = hidden.shape[0]
    catalog = lax.broadcasted_iota(jnp.int32, counts.shape, 1)
    own_count = jnp.sum(jnp.where(catalog == bucket_expert[0], counts, 0))
    position = lax.broadcasted_iota(jnp.int32, (rows_local, 1), 0)
    masked = jnp.where(position < own_count, hidden, jnp.zeros_like(hidden))
    total = lax.psum(own_count, ("dp", "expert")).astype(jnp.float32)
    divisor = jnp.float32(1.0)
    shard = lax.psum_scatter(
        block_product(masked, dout) / divisor, ("dp", "expert"), scatter_dimension=0, tiled=True
    )
    grad = shard / total
    blend = first_beta * momentum + (1.0 - first_beta) * grad
    direction = jnp.tanh(blend / soft_width) + decay_rate * param
    new_param = param - learn_rate * direction
    new_momentum = second_beta * momentum + (1.0 - second_beta) * grad
    return (new_param, new_momentum, direction)


def solution(mesh):
    in_specs = (
        P(("dp", "expert"), None),
        P(("dp", "expert"), None),
        P(("dp", "expert"), None),
        P(),
        P(("dp", "expert"), None),
        P(("dp", "expert"), None),
    )
    out_specs = (P(("dp", "expert"), None), P(("dp", "expert"), None), P(("dp", "expert"), None))
    return jax.shard_map(body, mesh=mesh, in_specs=in_specs, out_specs=out_specs, check_vma=False)
```

profile of v0, /device:TPU:0, one launch (start us, length us, event | category | flops | bytes accessed | tf_op | source)
XLA Modules:
  0.0 371.9 jit_solution(8885217002875847728)
XLA Ops:
  7.2 0.0 reduce-scatter.2.cloned.1.call-start
  7.9 1.3 fusion.4
  9.2 0.7 iota_compare_fusion
  9.8 30.7 %fusion = f32[1024,7168]{1,0:T(8,128)} fusion(bf16[1536,7168]{1,0:T(8,128)(2,1)} %param.7, bf16[1536,1024]{1,0:T(8,128)(2,1)} %param.6, pred[1536]{0:T(1024)(128)(4,1)S(1)} %iota_compare_fusion), kind=kOutput, calls=%fused_computation | convolution fusion | flops 22550151168 | bytes 54527488 | tf_op jit(solution)/shard_map/dot_general | solution.py:15
  40.6 0.0 copy-start
  40.6 0.0 copy-start.1
  40.6 0.0 reduce-scatter.2.cloned.1.call-update
  40.6 43.8 %psum.7 = s32[]{:T(128)} all-reduce(s32[]{:T(128)} %fusion.4), channel_id=1, replica_groups=mesh['dp'=4,'expert'=8] {'dp','expert'}, use_global_device_ids=true, to_apply=%region_2.3 | all-reduce | flops 1 | bytes 8 | tf_op jit(solution)/shard_map/psum | solution.py:24
  85.1 276.8 %reduce-scatter.2.cloned.1.call-done = f32[32,7168]{1,0:T(8,128)} async-done(((f32[1024,7168]{1,0:T(8,128)}), f32[32,7168]{1,0:T(8,128)}) %reduce-scatter.2.cloned.1.call-update) | async-done | bytes 917520 | tf_op jit(solution)/shard_map/reduce_scatter | solution.py:26
  361.9 0.0 copy-done
  361.9 0.0 copy-done.1
  361.9 3.1 multiply_subtract_fusion
Async XLA Ops:
  7.2 354.7 %reduce-scatter.2.cloned.1.call-start = ((), (), s32[]{:S(2)}) async-start(), calls=%async_computation.1 | async-start | bytes 30277632 | tf_op jit(solution)/shard_map/reduce_scatter | solution.py:26
  40.6 321.4 %copy-start = (f32[32,7168]{1,0:T(8,128)S(1)}, f32[32,7168]{1,0:T(8,128)}, u32[]{:S(2)}) copy-start(f32[32,7168]{1,0:T(8,128)} %param.10) | copy-start | bytes 2752516
  40.6 321.4 %copy-start.1 = (f32[32,7168]{1,0:T(8,128)S(1)}, f32[32,7168]{1,0:T(8,128)}, u32[]{:S(2)}) copy-start(f32[32,7168]{1,0:T(8,128)} %param.11) | copy-start | bytes 2752516
Sparse Core Ops, SparseCore 0:
  40.7 321.1 reduce-scatter.1
where the time goes:
time: 372 us
  waiting for transfers between devices  277 us (74%)
  blocking collectives  43.8 us (12%)
  matrix products  30.7 us (8%)
  between operations  15.3 us (4%)
  other arithmetic  5.06 us (1%)
    reduce_scatter x1, waiting for transfers between devices, body(): lax.psum_scatter(block_product(masked, dout) / divisor, ('dp', 'expert'),...  277 us
    psum x1, blocking collectives, body(): total = lax.psum(own_count, ('dp', 'expert')).astype(jnp.float32)  43.8 us
    dot_general x1, matrix products, block_product(): lax.dot_general(columns, dout, dims, preferred_element_type=jnp.float32)  30.7 us
  transfers between devices with their start and end apart: 1, of which 1 were waited for; matrix products, arithmetic and copies ran while one was open for 0% of the time, Pallas kernels for 0%

commit v1 on v0

v1 whole, which is shorter than its diff:
```python
import functools

import jax
import jax.numpy as jnp
from jax import lax
from jax.experimental import pallas as pl
from jax.experimental.pallas import tpu as pltpu
from jax.sharding import PartitionSpec as P

first_beta = 0.9
second_beta = 0.99
decay_rate = 0.1
learn_rate = 0.001
soft_width = 0.05

WIDTH = 256
LAGS = (2, 8, 13, 16, 19)
SLOTS = 3
HELD = LAGS[-1] + 1
MESH = pl.DeviceIdType.MESH


def block_product(columns, dout):
    dims = (((0,), (0,)), ((), ()))
    return lax.dot_general(columns, dout, dims, preferred_element_type=jnp.float32)


def mask_tokens(hidden, counts, bucket_expert):
    catalog = lax.broadcasted_iota(jnp.int32, counts.shape, 1)
    own_count = jnp.sum(jnp.where(catalog == bucket_expert[0], counts, 0))
    position = lax.broadcasted_iota(jnp.int32, (hidden.shape[0], 1), 0)
    return own_count, jnp.where(position < own_count, hidden, jnp.zeros_like(hidden))


def lion(grad, param, momentum):
    blend = first_beta * momentum + (1.0 - first_beta) * grad
    direction = jnp.tanh(blend / soft_width) + decay_rate * param
    new_param = param - learn_rate * direction
    new_momentum = second_beta * momentum + (1.0 - second_beta) * grad
    return (new_param, new_momentum, direction)


def plain_body(hidden, dout, counts, bucket_expert, param, momentum):
    own_count, masked = mask_tokens(hidden, counts, bucket_expert)
    total = lax.psum(own_count, ("dp", "expert")).astype(jnp.float32)
    shard = lax.psum_scatter(
        block_product(masked, dout), ("dp", "expert"), scatter_dimension=0, tiled=True
    )
    return lion(shard / total, param, momentum)


def reduce_kernel(
    chunks, ht_ref, dout_ref, count_ref, shard_ref, total_ref,
    acc, r0, r1, r2, r3, r4, tiles, count_in,
    tile_sem, send_sem, recv_sem, count_send, count_recv,
):
    rows = acc.shape[2]
    landing = (r0, r1, r2, r3, r4)
    dp = lax.axis_index("dp")
    ex = lax.axis_index("expert")
    y, x = lax.div(dp, 2), lax.rem(dp, 2)
    z1, z0, core = lax.div(ex, 4), lax.rem(lax.div(ex, 2), 2), lax.rem(ex, 2)
    step_x, step_y = 1 - 2 * x, 2 - 4 * y
    step_core, step_z0, step_z1 = 1 - 2 * core, 2 - 4 * z0, 4 - 8 * z1
    partners = (
        (dp, ex + step_core), (dp + step_x, ex), (dp + step_y, ex),
        (dp, ex + step_z0), (dp, ex + step_z1),
    )

    def tile_copy(c):
        slot = lax.rem(c, SLOTS)
        columns = pl.ds(pl.multiple_of(c * WIDTH, WIDTH), WIDTH)
        return pltpu.make_async_copy(
            dout_ref.at[:, columns], tiles.at[slot], tile_sem.at[slot]
        )

    def kind(c):
        z_first = lax.div(lax.rem(c, 4), 2) * (1 - lax.div(lax.div(c, 12) + 1, 2))
        return z_first, lax.rem(c, 2)

    def exchange(c, stage):
        half = landing[stage].shape[1]
        if stage == 0:
            target = (dp, ex + step_core)
        else:
            z_first, parity = kind(c)
            on_dp = z_first if stage >= 3 else 1 - z_first
            swap = parity if stage in (1, 3) else 1 - parity
            step_dp = (1 - swap) * step_x + swap * step_y
            step_ex = step_z0 if stage in (1, 3) else step_z1
            target = (dp + on_dp * step_dp, ex + (1 - on_dp) * step_ex)
        return pltpu.make_async_remote_copy(
            src_ref=acc.at[lax.rem(c, HELD), pl.ds(half, half)],
            dst_ref=landing[stage].at[c],
            send_sem=send_sem.at[stage, c],
            recv_sem=recv_sem.at[stage, c],
            device_id=target,
            device_id_type=MESH,
        )

    def count_exchange(stage):
        return pltpu.make_async_remote_copy(
            src_ref=count_in.at[stage],
            dst_ref=count_in.at[5 + stage],
            send_sem=count_send.at[stage],
            recv_sem=count_recv.at[stage],
            device_id=partners[stage],
            device_id_type=MESH,
        )

    for c in range(SLOTS):
        tile_copy(c).start()
    barrier = pltpu.get_barrier_semaphore()
    for partner in partners:
        pl.semaphore_signal(barrier, inc=1, device_id=partner, device_id_type=MESH)
    pl.semaphore_wait(barrier, 5)
    count_in[0] = count_ref[...]
    count_exchange(0).start()

    def multiply(c):
        tile_copy(c).wait()
        z_first, parity = kind(c)
        w_first, w_second = 8 - 6 * z_first, 4 - 3 * z_first
        w_x = (1 - parity) * w_first + parity * w_second
        w_y = parity * w_first + (1 - parity) * w_second
        w_z0, w_z1 = 2 + 6 * z_first, 1 + 3 * z_first
        mine = (y, x, z1, z0, core)
        weights = (w_y, w_x, w_z1, w_z0, 16)
        off = [
            [bit * weight for bit, weight in zip(mine, weights)],
            [(1 - bit) * weight for bit, weight in zip(mine, weights)],
        ]
        product = jnp.dot(
            ht_ref[...], tiles[lax.rem(c, SLOTS)], preferred_element_type=jnp.float32
        )
        held = lax.rem(c, HELD)
        for block in range(2 ** len(mine)):
            place = 0
            for i in range(len(mine)):
                place = place + off[(block >> (len(mine) - 1 - i)) & 1][i]
            acc[held, place] = product[block * rows:(block + 1) * rows]
        exchange(c, 0).start()

        @pl.when(c + SLOTS < chunks)
        def _():
            tile_copy(c + SLOTS).start()

    def fold(c, stage):
        half = landing[stage].shape[1]
        exchange(c, stage).wait_recv()
        held = lax.rem(c, HELD)
        acc[held, 0:half] = acc[held, 0:half] + landing[stage][c]
        exchange(c, stage + 1).start()

    def finish(c):
        exchange(c, 4).wait_recv()
        columns = pl.ds(pl.multiple_of(c * WIDTH, WIDTH), WIDTH)
        shard_ref[:, columns] = acc[lax.rem(c, HELD), 0] + r4[c, 0]
        for stage in range(5):
            exchange(c, stage).wait_send()

    def step(k, carry):
        @pl.when(k < chunks)
        def _():
            multiply(k)

        for stage in range(4):
            c = k - LAGS[stage]

            @pl.when((c >= 0) & (c < chunks))
            def _():
                fold(c, stage)

        c = k - LAGS[4]

        @pl.when(c >= 0)
        def _():
            finish(c)

        for stage in range(4):
            @pl.when(k == 3 * stage + 3)
            def _():
                count_exchange(stage).wait_recv()
                count_in[stage + 1] = count_in[stage] + count_in[5 + stage]
                count_exchange(stage + 1).start()

        return carry

    lax.fori_loop(0, chunks + LAGS[4], step, 0)
    count_exchange(4).wait_recv()
    total_ref[...] = count_in[4] + count_in[9]

    for stage in range(5):
        count_exchange(stage).wait_send()


def fast_body(devices, hidden, dout, counts, bucket_expert, param, momentum):
    own_count, masked = mask_tokens(hidden, counts, bucket_expert)
    tokens, features = hidden.shape
    width = dout.shape[1]
    rows = features // devices
    chunks = width // WIDTH
    spread = jnp.full((8, 128), own_count.astype(jnp.float32))
    vmem = pl.BlockSpec(memory_space=pltpu.VMEM)
    shard, total = pl.pallas_call(
        functools.partial(reduce_kernel, chunks),
        out_shape=(
            jax.ShapeDtypeStruct((rows, width), jnp.float32),
            jax.ShapeDtypeStruct((8, 128), jnp.float32),
        ),
        in_specs=[vmem, pl.BlockSpec(memory_space=pl.ANY), vmem],
        out_specs=(vmem, vmem),
        scratch_shapes=[pltpu.VMEM((HELD, devices, rows, WIDTH), jnp.float32)]
        + [
            pltpu.VMEM((chunks, devices >> (s + 1), rows, WIDTH), jnp.float32)
            for s in range(5)
        ]
        + [
            pltpu.VMEM((SLOTS, tokens, WIDTH), jnp.bfloat16),
            pltpu.VMEM((10, 8, 128), jnp.float32),
            pltpu.SemaphoreType.DMA((SLOTS,)),
            pltpu.SemaphoreType.DMA((5, chunks)),
            pltpu.SemaphoreType.DMA((5, chunks)),
            pltpu.SemaphoreType.DMA((5,)),
            pltpu.SemaphoreType.DMA((5,)),
        ],
        compiler_params=pltpu.CompilerParams(
            collective_id=0, has_side_effects=True, vmem_limit_bytes=67043328
        ),
    )(masked.T, dout, spread)
    return lion(shard / total[0, 0], param, momentum)


def solution(mesh):
    spec = P(("dp", "expert"), None)
    in_specs = (spec, spec, spec, P(), spec, spec)
    out_specs = (spec, spec, spec)
    if mesh.shape["dp"] == 4 and mesh.shape["expert"] == 8:
        body = functools.partial(fast_body, mesh.size)
    else:
        body = plain_body
    return jax.shard_map(body, mesh=mesh, in_specs=in_specs, out_specs=out_specs, check_vma=False)
```

time: 372 us -> 165 us (0.44)
  waiting for transfers between devices: 277 us -> 0 us
  Pallas kernels: 0 us -> 146 us
  blocking collectives: 43.8 us -> 0 us
  matrix products: 30.7 us -> 0 us
  between operations: 15.3 us -> 1.95 us
  local copies, waits for them, and re-layouts: 0.01 us -> 5.05 us
    reduce_scatter x1 -> x0, waiting for transfers between devices: 277 us -> none  [body(): lax.psum_scatter(block_product(masked, dout) / divisor, ('dp', 'expert'),...]
    pallas_call x0 -> x1, Pallas kernels: none -> 146 us  [fast_body(): pl.pallas_call(functools.partial(reduce_kernel, chunks), out_shape=(jax.S...]
    psum x1 -> x0, blocking collectives: 43.8 us -> none  [body(): total = lax.psum(own_count, ('dp', 'expert')).astype(jnp.float32)]
    dot_general x1 -> x0, matrix products: 30.7 us -> none  [block_product(): lax.dot_general(columns, dout, dims, preferred_element_type=jnp.float32)]
  transfers between devices with their start and end apart: 1 -> 0, of which waited for: 1 -> 0; matrix products, arithmetic and copies ran while one was open for 0% -> 0% of each run, Pallas kernels for 0% -> 0%
where the time goes in v1:
time: 165 us; the launch traced here: 161 us
  Pallas kernels  146 us (88%)
  other arithmetic  8.18 us (5%)
  local copies, waits for them, and re-layouts  5.05 us (3%)
  between operations  1.95 us (1%)
    pallas_call x1, Pallas kernels, fast_body(): pl.pallas_call(functools.partial(reduce_kernel, chunks), out_shape=(jax.S...  146 us
    sub x1, other arithmetic, lion(): new_param = param - learn_rate * direction  4.33 us

profile of v1, /device:TPU:0, one launch (start us, length us, event | category | flops | bytes accessed | tf_op | source)
XLA Modules:
  0.0 161.4 jit_solution(1146794233781345149)
XLA Ops:
  1.3 1.3 fusion
  3.2 0.7 iota_compare_fusion
  3.9 0.6 broadcast_in_dim.21.count_ref
  4.5 3.2 %copy.9 = bf16[1536,1024]{0,1:T(8,128)(2,1)S(1)} copy(bf16[1536,1024]{1,0:T(8,128)(2,1)} %param.6) | data formatting | bytes 6291456 | tf_op args[0]
  7.7 1.9 %select_bitcast_fusion.ht_ref = bf16[1024,1536]{1,0:T(8,128)(2,1)} fusion(bf16[1536,1024]{0,1:T(8,128)(2,1)S(1)} %copy.9, pred[1536]{0:T(1024)(128)(4,1)S(1)} %iota_compare_fusion), kind=kLoop, calls=%fused_computation | loop fusion | flops 1572864 | bytes 6292992 | tf_op jit(solution)/shard_map/transpose | solution.py:230
  9.6 146.3 %shard_map.85 = (f32[32,7168]{1,0:T(8,128)}, f32[8,128]{1,0:T(8,128)}) custom-call(bf16[1024,1536]{1,0:T(8,128)(2,1)} %select_bitcast_fusion.ht_ref, bf16[1536,7168]{1,0:T(8,128)(2,1)} %dout_ref.1, f32[8,128]{1,0:T(8,128)} %broadcast_in_dim.21.count_ref), custom_call_target="tpu_custom_call" | custom-call | tf_op jit(solution)/shard_map/pallas_call | solution.py:205
  155.8 1.3 slice.3
  157.1 4.3 %multiply_subtract_fusion = (f32[32,7168]{1,0:T(8,128)}, f32[32,7168]{1,0:T(8,128)}, f32[32,7168]{1,0:T(8,128)}) fusion(f32[32,7168]{1,0:T(8,128)} %param.10, f32[32,7168]{1,0:T(8,128)} %get-tuple-element.5, f32[]{:T(128)} %bitcast.2, f32[32,7168]{1,0:T(8,128)} %param.11), kind=kLoop, calls=%fused_computation.2 | loop fusion | flops 2752512 | bytes 5505028 | tf_op jit(solution)/shard_map/sub | solution.py:38

commit v2 on v1

--- a/solution.py
+++ b/solution.py
@@ -14,7 +14,7 @@
 soft_width = 0.05
 
 WIDTH = 256
-LAGS = (2, 8, 13, 16, 19)
+LAGS = (2, 10, 16, 20, 23)
 SLOTS = 3
 HELD = LAGS[-1] + 1
 MESH = pl.DeviceIdType.MESH
@@ -75,7 +75,7 @@
         )
 
     def kind(c):
-        z_first = lax.div(lax.rem(c, 4), 2) * (1 - lax.div(lax.div(c, 12) + 1, 2))
+        z_first = lax.div(lax.rem(c, 9), 7)
         return z_first, lax.rem(c, 2)
 
     def exchange(c, stage):

time: 165 us -> 147 us (0.89); the launches traced: 161 us -> 147 us
  Pallas kernels: 146 us -> 132 us
    pallas_call x1, Pallas kernels: 146 us -> 132 us  [fast_body(): pl.pallas_call(functools.partial(reduce_kernel, chunks), out_shape=(jax.S...]
where the time goes in v2:
time: 147 us
  Pallas kernels  132 us (90%)
  other arithmetic  8.18 us (6%)
  local copies, waits for them, and re-layouts  5.05 us (3%)
  between operations  1.95 us (1%)
    pallas_call x1, Pallas kernels, fast_body(): pl.pallas_call(functools.partial(reduce_kernel, chunks), out_shape=(jax.S...  132 us
    sub x1, other arithmetic, lion(): new_param = param - learn_rate * direction  4.33 us
    unnamed x1, local copies, waits for them, and re-layouts  3.18 us

profile of v2, /device:TPU:0, one launch (start us, length us, event | category | flops | bytes accessed | tf_op | source)
XLA Modules:
  0.0 146.8 jit_solution(2228395056465532160)
XLA Ops:
  1.3 1.3 fusion
  3.2 0.7 iota_compare_fusion
  3.9 0.6 broadcast_in_dim.21.count_ref
  4.5 3.2 %copy.9 = bf16[1536,1024]{0,1:T(8,128)(2,1)S(1)} copy(bf16[1536,1024]{1,0:T(8,128)(2,1)} %param.6) | data formatting | bytes 6291456 | tf_op args[0]
  7.7 1.9 %select_bitcast_fusion.ht_ref = bf16[1024,1536]{1,0:T(8,128)(2,1)} fusion(bf16[1536,1024]{0,1:T(8,128)(2,1)S(1)} %copy.9, pred[1536]{0:T(1024)(128)(4,1)S(1)} %iota_compare_fusion), kind=kLoop, calls=%fused_computation | loop fusion | flops 1572864 | bytes 6292992 | tf_op jit(solution)/shard_map/transpose | solution.py:230
  9.6 131.7 %shard_map.85 = (f32[32,7168]{1,0:T(8,128)}, f32[8,128]{1,0:T(8,128)}) custom-call(bf16[1024,1536]{1,0:T(8,128)(2,1)} %select_bitcast_fusion.ht_ref, bf16[1536,7168]{1,0:T(8,128)(2,1)} %dout_ref.1, f32[8,128]{1,0:T(8,128)} %broadcast_in_dim.21.count_ref), custom_call_target="tpu_custom_call" | custom-call | tf_op jit(solution)/shard_map/pallas_call | solution.py:205
  141.2 1.3 slice.3
  142.5 4.3 %multiply_subtract_fusion = (f32[32,7168]{1,0:T(8,128)}, f32[32,7168]{1,0:T(8,128)}, f32[32,7168]{1,0:T(8,128)}) fusion(f32[32,7168]{1,0:T(8,128)} %param.10, f32[32,7168]{1,0:T(8,128)} %get-tuple-element.5, f32[]{:T(128)} %bitcast.2, f32[32,7168]{1,0:T(8,128)} %param.11), kind=kLoop, calls=%fused_computation.2 | loop fusion | flops 2752512 | bytes 5505028 | tf_op jit(solution)/shard_map/sub | solution.py:38
